TPU v7x, 32 devices: a whole 2x2x4 slice. The times are simulated.
32 devices in a mesh: groups: 2 (over y), tok: 4 (over z), lat: 2 (over x), rep: 2 (over core).
Axes of the slice: x: 2, y: 2, z: 4, core: 2. Of those that a mesh axis runs over, the one named last changes fastest.
Arguments:
- tokens: bfloat16 [2048, 512], P(('groups', 'tok', 'lat')), parts along dimension 0, may hold values from -15 to 15
- latents: bfloat16 [768, 512], P(('tok', 'lat')), may hold values from -6 to 6
- w_tok: bfloat16 [1, 512, 2, 512], P(None, None, None, 'rep'), may hold values from -1.5 to 1.5
- w_lat: bfloat16 [1, 512, 2, 512], P(None, None, None, 'rep'), may hold values from -1.5 to 1.5
- o_tok: bfloat16 [1, 512, 512], P(None, 'rep'), may hold values from -0.25 to 0.25
- o_lat: bfloat16 [1, 512, 512], P(None, 'rep'), may hold values from -0.25 to 0.25
- g_tok: float32 [1, 512], replicated, may hold values from 0.1 to 1.9
- g_lat: float32 [1, 512], replicated, may hold values from 0.1 to 1.9
Outputs:
- tokens_out: bfloat16 [2048, 512], P(('groups', 'tok', 'lat')), parts along dimension 0
- latents_out: bfloat16 [1536, 512], P(('groups', 'tok', 'lat')), parts along dimension 0
There are 2 independent parts, one for each index of `groups`. A program takes and returns all parts, laid end to end along the dimension named above; an argument that names none is the same for every part. Nothing has to cross between parts.
All inputs are finite; a program needn't handle non-finite values.
Results may differ from a plain program's by a relative error of at most 0.0068.
Values may be sent and summed in bfloat16 or wider, within the bound.
A program may use at most 64 MiB of HBM per device.

v0:
```python
import functools

import jax
import jax.numpy as jnp
from jax import lax
from jax.experimental import pallas as pl
from jax.experimental.pallas import tpu as pltpu
from jax.sharding import PartitionSpec as P

D = 512
HEADS = 8


EPS = 1e-06


def rms_scale(source, gain_row):
    widened = source.astype(jnp.float32)
    mean_sq = jnp.mean(widened * widened, axis=-1, keepdims=True)
    return (widened * lax.rsqrt(mean_sq + EPS) * gain_row).astype(jnp.bfloat16)


def head_terms(per_head):
    tok_key, tok_val, lat_key, lat_val = per_head
    scale = lat_key.shape[1] ** (-0.5)
    scores = (
        lax.dot_general(
            lat_key, tok_key, (((1,), (1,)), ((), ())), preferred_element_type=jnp.float32
        )
        * scale
    )
    peak_tok = jnp.max(scores, axis=0, keepdims=True)
    tok_exp = jnp.exp(scores - peak_tok)
    tok_weights = (tok_exp / jnp.sum(tok_exp, axis=0, keepdims=True)).astype(jnp.bfloat16)
    tok_att = lax.dot_general(
        tok_weights, lat_val, (((0,), (0,)), ((), ())), preferred_element_type=jnp.float32
    )
    peak_lat = jnp.max(scores, axis=1)
    lat_exp = jnp.exp(scores - peak_lat[:, None])
    block_den = jnp.sum(lat_exp, axis=1)
    block_num = jnp.dot(lat_exp.astype(jnp.bfloat16), tok_val, preferred_element_type=jnp.float32)
    return (tok_att.astype(jnp.bfloat16), block_num, block_den, peak_lat)


def body(tokens, latents, w_tok, w_lat, o_tok, o_lat, g_tok, g_lat):
    head_size = D // HEADS
    row_count = tokens.shape[0]
    model_width = tokens.shape[1]
    half_width = w_tok.shape[3]
    head_count = half_width // head_size
    tok_in = rms_scale(tokens, g_tok[0])
    lat_in = rms_scale(latents, g_lat[0])
    tok_proj = jnp.dot(
        tok_in, w_tok[0].reshape(model_width, 2 * half_width), preferred_element_type=jnp.float32
    )
    tok_proj = tok_proj.astype(jnp.bfloat16).reshape(row_count, 2, head_count, head_size)
    lat_own = jnp.dot(
        lat_in, w_lat[0].reshape(model_width, 2 * half_width), preferred_element_type=jnp.float32
    )
    lat_own = lat_own.astype(jnp.bfloat16).reshape(-1, 2, half_width)
    lat_proj = lax.all_gather(lat_own, ("tok", "lat"), axis=0, tiled=True)
    lat_count = lat_proj.shape[0]
    lat_proj = lat_proj.reshape(lat_count, 2, head_count, head_size)
    per_head = (
        jnp.transpose(tok_proj[:, 0], (1, 0, 2)),
        jnp.transpose(tok_proj[:, 1], (1, 0, 2)),
        jnp.transpose(lat_proj[:, 0], (1, 0, 2)),
        jnp.transpose(lat_proj[:, 1], (1, 0, 2)),
    )
    tok_att, block_num, block_den, peaks = lax.map(head_terms, per_head)
    tok_att = jnp.transpose(tok_att, (1, 0, 2)).reshape(row_count, half_width)
    block_num = jnp.transpose(block_num, (1, 0, 2))
    block_den = jnp.transpose(block_den)
    peaks = jnp.transpose(peaks)
    got_num = lax.all_to_all(
        block_num.reshape(lat_count, half_width),
        ("tok", "lat"),
        split_axis=0,
        concat_axis=0,
        tiled=True,
    )
    got_den = lax.all_to_all(block_den, ("tok", "lat"), split_axis=0, concat_axis=0, tiled=True)
    got_peak = lax.all_to_all(peaks, ("tok", "lat"), split_axis=0, concat_axis=0, tiled=True)
    sources = lax.axis_size(("tok", "lat"))
    got_num = got_num.reshape(sources, -1, head_count, head_size)
    got_den = got_den.reshape(sources, -1, head_count)
    got_peak = got_peak.reshape(sources, -1, head_count)
    score_top = jnp.max(got_peak, axis=0)
    factor = jnp.exp(got_peak - score_top)
    num_own = jnp.sum(got_num * factor[:, :, :, None], axis=0)
    den_own = jnp.sum(got_den * factor, axis=0)
    lat_att = (num_own / den_own[:, :, None]).astype(jnp.bfloat16).reshape(-1, half_width)
    lat_part = jnp.dot(lat_att, o_lat[0], preferred_element_type=jnp.float32)
    lat_sum = lax.psum(lat_part, "rep")
    latents = (latents.astype(jnp.float32) + lat_sum).astype(jnp.bfloat16)
    tok_part = jnp.dot(tok_att, o_tok[0], preferred_element_type=jnp.float32)
    tok_sum = lax.psum(tok_part, "rep")
    tokens = (tokens.astype(jnp.float32) + tok_sum).astype(jnp.bfloat16)
    return (tokens, latents)


MESH_ID= pl.DeviceIdType.MESH
UP, DOWN, ACROSS, PARTNER = 0, 1, 2, 3


def attend(query, key_ref, value_ref, head_size):
    lanes = 2 * head_size
    rows = query.shape[0]
    outs = []
    for start in range(0, query.shape[1], lanes):
        pair = query[:, start : start + lanes]
        first = lax.broadcasted_iota(jnp.int32, pair.shape, 1) < head_size
        zero = jnp.zeros_like(pair)
        stacked = jnp.concatenate(
            [jnp.where(first, pair, zero), jnp.where(first, zero, pair)], axis=0
        )
        stacked = stacked * jnp.asarray(head_size ** (-0.5), stacked.dtype)
        scores = lax.dot_general(
            stacked,
            key_ref[:, start : start + lanes],
            (((1,), (1,)), ((), ())),
            preferred_element_type=jnp.float32,
        )
        peak = jnp.max(scores, axis=1, keepdims=True)
        weights = jnp.exp(scores - peak)
        total = jnp.sum(weights, axis=1, keepdims=True)
        mixed = jnp.dot(
            weights.astype(jnp.bfloat16),
            value_ref[:, start : start + lanes],
            preferred_element_type=jnp.float32,
        )
        mixed = mixed / total
        outs.append(jnp.where(first, mixed[:rows], mixed[rows:]))
    return jnp.concatenate(outs, axis=1).astype(jnp.bfloat16)


def kernel(
    depth,
    wide,
    tok_ref,
    lat_ref,
    w_tok_hbm,
    w_lat_hbm,
    o_tok_hbm,
    o_lat_hbm,
    g_tok_ref,
    g_lat_ref,
    tok_out,
    lat_out,
    tok_all,
    lat_all,
    w_tok_ref,
    w_lat_ref,
    o_ref,
    tok_key,
    tok_val,
    lat_key,
    lat_val,
    tok_att,
    lat_att,
    send_sem,
    recv_sem,
    load_sem,
    o_send,
    o_recv,
    att_send,
    att_recv,
):
    z = lax.axis_index("tok")
    x = lax.axis_index("lat")
    core = lax.axis_index("rep")
    across = 1 - x
    tok_rows, width = tok_ref.shape
    lat_rows = lat_ref.shape[0]
    half_width = tok_key.shape[1]
    head_size = D // HEADS
    me = z * wide + x
    devices = {
        UP: {"tok": z + 1},
        DOWN: {"tok": z - 1},
        ACROSS: {"lat": across},
        PARTNER: {"rep": 1 - core},
    }
    has_up = z + 1 < depth
    has_down = z > 0

    barrier = pltpu.get_barrier_semaphore()

    def greet(way):
        pl.semaphore_signal(barrier, inc=1, device_id=devices[way], device_id_type=MESH_ID)

    pl.when(has_up)(lambda: greet(UP))
    pl.when(has_down)(lambda: greet(DOWN))
    greet(ACROSS)
    greet(PARTNER)

    loads = [
        pltpu.make_async_copy(w_lat_hbm, w_lat_ref, load_sem.at[0]),
        pltpu.make_async_copy(w_tok_hbm, w_tok_ref, load_sem.at[1]),
        pltpu.make_async_copy(
            o_lat_hbm, o_ref.at[0, pl.ds(core * half_width, half_width)], load_sem.at[2]
        ),
        pltpu.make_async_copy(
            o_tok_hbm, o_ref.at[1, pl.ds(core * half_width, half_width)], load_sem.at[3]
        ),
    ]
    for load in loads:
        load.start()

    pl.semaphore_wait(barrier, 2 + has_up.astype(jnp.int32) + has_down.astype(jnp.int32))

    sizes = (lat_rows, tok_rows)
    own = (lat_ref, tok_ref)
    gathered = (lat_all, tok_all)

    def part(kind, block, half):
        rows = sizes[kind] // 2
        start = pl.multiple_of(block * sizes[kind] + half * rows, 16)
        return gathered[kind].at[pl.ds(start, rows)]

    def piece(kind, block, way, mine=False):
        rows = sizes[kind] // 2
        target = part(kind, block, core)
        source = target
        if mine:
            source = own[kind].at[pl.ds(pl.multiple_of(core * rows, 16), rows)]
        return pltpu.make_async_remote_copy(
            src_ref=source,
            dst_ref=target,
            send_sem=send_sem.at[way, kind, block],
            recv_sem=recv_sem.at[core, kind, block],
            device_id=devices[way],
            device_id_type=MESH_ID,
        )

    def landed(kind, block, half):
        target = part(kind, block, half)
        pltpu.make_async_copy(target, target, recv_sem.at[half, kind, block]).wait()

    def each_way(ways, act):
        for way in ways:
            if way == UP:
                pl.when(has_up)(lambda: act(UP))
            elif way == DOWN:
                pl.when(has_down)(lambda: act(DOWN))
            else:
                act(way)

    events = []
    for k in range(depth - 1):
        events.append((z - 1 - k, z - 1 - k >= 0, x, (UP, ACROSS, PARTNER)))
        events.append((z + 1 + k, z + 1 + k < depth, x, (DOWN, ACROSS, PARTNER)))
        if k == 0:
            events.append((z, None, across, (PARTNER,)))
        else:
            events.append((z - k, z - k >= 0, across, (PARTNER,)))
            events.append((z + k, z + k < depth, across, (PARTNER,)))
    last = depth - 1
    events.append((z - last, z - last >= 0, across, (PARTNER,)))
    events.append((z + last, z + last < depth, across, (PARTNER,)))

    for kind in range(2):
        each_way((UP, DOWN, ACROSS), lambda way: piece(kind, me, way, True).start())

    o_copies = [
        pltpu.make_async_remote_copy(
            src_ref=hbm,
            dst_ref=o_ref.at[i, pl.ds(core * half_width, half_width)],
            send_sem=o_send.at[i],
            recv_sem=o_recv.at[i],
            device_id=devices[PARTNER],
            device_id_type=MESH_ID,
        )
        for i, hbm in enumerate((o_lat_hbm, o_tok_hbm))
    ]
    for copy in o_copies:
        copy.start()

    weights = (w_lat_ref, w_tok_ref)
    gains = (g_lat_ref, g_tok_ref)
    keys = (lat_key, tok_key)
    values = (lat_val, tok_val)

    def project(kind, block, source):
        normed = rms_scale(source, gains[kind][...])
        both = jnp.dot(normed, weights[kind][...], preferred_element_type=jnp.float32)
        rows = pl.ds(pl.multiple_of(block * sizes[kind], 16), sizes[kind])
        both = both.astype(jnp.bfloat16)
        keys[kind][rows, :] = both[:, :half_width]
        values[kind][rows, :] = both[:, half_width:]
        return both[:, :half_width]

    queries = []
    for kind in range(2):
        loads[kind].wait()
        queries.append(project(kind, me, own[kind][...]))

    for row, exists, column, ways in events:
        block = row * wide + column

        def relay(block=block, ways=ways):
            for kind in range(2):
                landed(kind, block, core)
                each_way(ways, lambda way: piece(kind, block, way).start())

        if exists is None:
            relay()
        else:
            pl.when(exists)(relay)

    def take(step, carry):
        block = lax.rem(me + step, depth * wide)
        for kind in range(2):
            landed(kind, block, 1 - core)
            rows = pl.ds(pl.multiple_of(block * sizes[kind], 16), sizes[kind])
            project(kind, block, gathered[kind][rows, :])
        return carry

    lax.fori_loop(1, depth * wide, take, 0)

    mine = pl.ds(pl.multiple_of(core * half_width, 128), half_width)
    attended = (lat_att, tok_att)
    att_copies = []
    for kind in range(2):
        attended[kind][core] = attend(queries[kind], keys[1 - kind], values[1 - kind], head_size)
        copy = pltpu.make_async_remote_copy(
            src_ref=attended[kind].at[core],
            dst_ref=attended[kind].at[core],
            send_sem=att_send.at[kind],
            recv_sem=att_recv.at[kind],
            device_id=devices[PARTNER],
            device_id_type=MESH_ID,
        )
        copy.start()
        att_copies.append(copy)

    outs = (lat_out, tok_out)
    for kind in range(2):
        loads[2 + kind].wait()
        o_copies[kind].wait()
        att_copies[kind].wait()
        total = own[kind][...].astype(jnp.float32)
        for half in range(2):
            total += jnp.dot(
                attended[kind][half],
                o_ref[kind, half * half_width : (half + 1) * half_width, :],
                preferred_element_type=jnp.float32,
            )
        outs[kind][...] = total.astype(jnp.bfloat16)

    for kind in range(2):
        each_way((UP, DOWN, ACROSS), lambda way: piece(kind, me, way, True).wait_send())
    for row, exists, column, ways in events:
        block = row * wide + column

        def drain(block=block, ways=ways):
            for kind in range(2):
                each_way(ways, lambda way: piece(kind, block, way).wait_send())

        if exists is None:
            drain()
        else:
            pl.when(exists)(drain)


def gathered_body(tokens, latents, w_tok, w_lat, o_tok, o_lat, g_tok, g_lat):
    depth = lax.axis_size("tok")
    wide = lax.axis_size("lat")
    tok_rows, width = tokens.shape
    lat_rows = latents.shape[0]
    half_width = w_tok.shape[3]
    blocks = depth * wide
    bf16 = jnp.bfloat16
    vmem = pl.BlockSpec(memory_space=pltpu.VMEM)
    hbm = pl.BlockSpec(memory_space=pl.ANY)
    dma = pltpu.SemaphoreType.DMA
    return pl.pallas_call(
        functools.partial(kernel, depth, wide),
        out_shape=(
            jax.ShapeDtypeStruct(tokens.shape, bf16),
            jax.ShapeDtypeStruct(latents.shape, bf16),
        ),
        in_specs=[vmem, vmem, hbm, hbm, hbm, hbm, vmem, vmem],
        out_specs=(vmem, vmem),
        scratch_shapes=[
            pltpu.VMEM((blocks * tok_rows, width), bf16),
            pltpu.VMEM((blocks * lat_rows, width), bf16),
            pltpu.VMEM((width, 2 * half_width), bf16),
            pltpu.VMEM((width, 2 * half_width), bf16),
            pltpu.VMEM((2, 2 * half_width, width), bf16),
            pltpu.VMEM((blocks * tok_rows, half_width), bf16),
            pltpu.VMEM((blocks * tok_rows, half_width), bf16),
            pltpu.VMEM((blocks * lat_rows, half_width), bf16),
            pltpu.VMEM((blocks * lat_rows, half_width), bf16),
            pltpu.VMEM((2, tok_rows, half_width), bf16),
            pltpu.VMEM((2, lat_rows, half_width), bf16),
            dma((4, 2, blocks)),
            dma((2, 2, blocks)),
            dma((4,)),
            dma((2,)),
            dma((2,)),
            dma((2,)),
            dma((2,)),
        ],
        compiler_params=pltpu.CompilerParams(
            collective_id=0, has_side_effects=True, vmem_limit_bytes=48 * 1024 * 1024
        ),
    )(
        tokens,
        latents,
        w_tok[0].reshape(width, 2 * half_width),
        w_lat[0].reshape(width, 2 * half_width),
        o_tok[0],
        o_lat[0],
        g_tok,
        g_lat,
    )


def solution(mesh):
    placed = (
        P(("groups", "tok", "lat"), None),
        P(("tok", "lat"), None),
        P(None, None, None, "rep"),
        P(None, None, None, "rep"),
        P(None, "rep", None),
        P(None, "rep", None),
        P(),
        P(),
    )
    sizes = dict(mesh.shape)
    resident = sizes["lat"] == 2 and sizes["rep"] == 2 and 2 <= sizes["tok"] <= 4
    return jax.shard_map(
        gathered_body if resident else body,
        mesh=mesh,
        in_specs=placed,
        out_specs=(P(("groups", "tok", "lat"), None), P(("groups", "tok", "lat"), None)),
        check_vma=False,
    )
```

profile of v0, /device:TPU:1, one launch (start us, length us, event | category | flops | bytes accessed | tf_op | source)
XLA Modules:
  0.0 31.4 jit_solution(16957152411904452161)
XLA Ops:
  0.6 0.0 copy-start.6
  0.6 1.2 %copy.10 = bf16[64,8,2,256]{3,1,2,0:T(8,128)(2,1)S(1)} copy(bf16[64,8,2,256]{3,2,1,0:T(2,128)(2,1)} %bitcast.12) | data formatting | bytes 1048576
  1.8 0.0 copy-done.6
  1.8 0.0 copy-start
  1.9 0.0 copy-start.1
  1.9 0.0 copy-start.2
  1.9 0.0 copy-start.3
  1.9 0.0 copy-start.4
  1.9 0.0 copy-start.5
  1.9 0.1 copy.11
  2.0 0.8 %copy-done = bf16[1,256,512]{2,1,0:T(8,128)(2,1)S(1)} copy-done((bf16[1,256,512]{2,1,0:T(8,128)(2,1)S(1)}, bf16[1,256,512]{2,1,0:T(8,128)(2,1)}, u32[]{:S(2)}) %copy-start) | copy-done | bytes 262168
  2.8 0.1 copy-done.1
  2.9 0.0 copy-done.2
  2.9 0.0 copy-done.3
  2.9 0.0 copy-done.4
  2.9 0.0 copy-done.5
  2.9 27.1 %shard_map.95 = (bf16[128,512]{1,0:T(8,128)(2,1)S(1)}, bf16[96,512]{1,0:T(8,128)(2,1)S(1)}) custom-call(bf16[128,512]{1,0:T(8,128)(2,1)S(1)} %copy-done.2, bf16[96,512]{1,0:T(8,128)(2,1)S(1)} %copy-done.3, bf16[512,512]{1,0:T(8,128)(2,1)S(1)} %bitcast.8, bf16[512,512]{1,0:T(8,128)(2,1)S(1)} %bitcast.9, bf16[256,512]{1,0:T(8,128)(2,1)S(1)} %bitcast.10, ...), custom_call_target="tpu_custom_call" | custom-call | tf_op jit(solution)/shard_map/pallas_call | solution.py:377
  30.1 0.7 %copy.14 = bf16[128,512]{1,0:T(8,128)(2,1)} copy(bf16[128,512]{1,0:T(8,128)(2,1)S(1)} %get-tuple-element.4) | data formatting | bytes 262144
  30.8 0.6 %copy.15 = bf16[96,512]{1,0:T(8,128)(2,1)} copy(bf16[96,512]{1,0:T(8,128)(2,1)S(1)} %get-tuple-element.5) | data formatting | bytes 196608
Async XLA Ops:
  0.6 1.2 %copy-start.6 = (bf16[1,512,2,256]{3,2,1,0:T(2,128)(2,1)S(1)}, bf16[1,512,2,256]{3,2,1,0:T(2,128)(2,1)}, u32[]{:S(2)}) copy-start(bf16[1,512,2,256]{3,2,1,0:T(2,128)(2,1)} %param.11) | copy-start | bytes 1572868
  1.8 1.0 %copy-start = (bf16[1,256,512]{2,1,0:T(8,128)(2,1)S(1)}, bf16[1,256,512]{2,1,0:T(8,128)(2,1)}, u32[]{:S(2)}) copy-start(bf16[1,256,512]{2,1,0:T(8,128)(2,1)} %param.12) | copy-start | bytes 786436
  1.9 1.0 %copy-start.1 = (bf16[1,256,512]{2,1,0:T(8,128)(2,1)S(1)}, bf16[1,256,512]{2,1,0:T(8,128)(2,1)}, u32[]{:S(2)}) copy-start(bf16[1,256,512]{2,1,0:T(8,128)(2,1)} %param.13) | copy-start | bytes 786436
  1.9 1.0 %copy-start.2 = (bf16[128,512]{1,0:T(8,128)(2,1)S(1)}, bf16[128,512]{1,0:T(8,128)(2,1)}, u32[]{:S(2)}) copy-start(bf16[128,512]{1,0:T(8,128)(2,1)} %tok_ref.1) | copy-start | bytes 393220
  1.9 1.1 %copy-start.3 = (bf16[96,512]{1,0:T(8,128)(2,1)S(1)}, bf16[96,512]{1,0:T(8,128)(2,1)}, u32[]{:S(2)}) copy-start(bf16[96,512]{1,0:T(8,128)(2,1)} %lat_ref.1) | copy-start | bytes 294916
  1.9 1.1 %copy-start.4 = (f32[1,512]{1,0:T(1,128)S(1)}, f32[1,512]{1,0:T(1,128)}, u32[]{:S(2)}) copy-start(f32[1,512]{1,0:T(1,128)} %g_tok_ref.1) | copy-start | bytes 6148
  1.9 1.0 %copy-start.5 = (f32[1,512]{1,0:T(1,128)S(1)}, f32[1,512]{1,0:T(1,128)}, u32[]{:S(2)}) copy-start(f32[1,512]{1,0:T(1,128)} %g_lat_ref.1) | copy-start | bytes 6148
where the time goes:
time: 31.7 us; the launch traced here: 31.4 us
  Pallas kernels  27.1 us (85%)
  local copies, waits for them, and re-layouts  3.53 us (11%)
  between operations  0.72 us (2%)
    pallas_call x1, Pallas kernels, gathered_body(): pl.pallas_call(functools.partial(kernel, depth, wide), out_shape=(jax.Sha...  27.1 us
    unnamed x18, local copies, waits for them, and re-layouts  3.53 us

commit v1 on v0

v1 whole, which is shorter than its diff:
```python
import functools

import jax
import jax.numpy as jnp
from jax import lax
from jax.experimental import pallas as pl
from jax.experimental.pallas import tpu as pltpu
from jax.sharding import PartitionSpec as P

D = 512
HEADS = 8


EPS = 1e-06


def rms_scale(source, gain_row):
    widened = source.astype(jnp.float32)
    mean_sq = jnp.mean(widened * widened, axis=-1, keepdims=True)
    return (widened * lax.rsqrt(mean_sq + EPS) * gain_row).astype(jnp.bfloat16)


def head_terms(per_head):
    tok_key, tok_val, lat_key, lat_val = per_head
    scale = lat_key.shape[1] ** (-0.5)
    scores = (
        lax.dot_general(
            lat_key, tok_key, (((1,), (1,)), ((), ())), preferred_element_type=jnp.float32
        )
        * scale
    )
    peak_tok = jnp.max(scores, axis=0, keepdims=True)
    tok_exp = jnp.exp(scores - peak_tok)
    tok_weights = (tok_exp / jnp.sum(tok_exp, axis=0, keepdims=True)).astype(jnp.bfloat16)
    tok_att = lax.dot_general(
        tok_weights, lat_val, (((0,), (0,)), ((), ())), preferred_element_type=jnp.float32
    )
    peak_lat = jnp.max(scores, axis=1)
    lat_exp = jnp.exp(scores - peak_lat[:, None])
    block_den = jnp.sum(lat_exp, axis=1)
    block_num = jnp.dot(lat_exp.astype(jnp.bfloat16), tok_val, preferred_element_type=jnp.float32)
    return (tok_att.astype(jnp.bfloat16), block_num, block_den, peak_lat)


def body(tokens, latents, w_tok, w_lat, o_tok, o_lat, g_tok, g_lat):
    head_size = D // HEADS
    row_count = tokens.shape[0]
    model_width = tokens.shape[1]
    half_width = w_tok.shape[3]
    head_count = half_width // head_size
    tok_in = rms_scale(tokens, g_tok[0])
    lat_in = rms_scale(latents, g_lat[0])
    tok_proj = jnp.dot(
        tok_in, w_tok[0].reshape(model_width, 2 * half_width), preferred_element_type=jnp.float32
    )
    tok_proj = tok_proj.astype(jnp.bfloat16).reshape(row_count, 2, head_count, head_size)
    lat_own = jnp.dot(
        lat_in, w_lat[0].reshape(model_width, 2 * half_width), preferred_element_type=jnp.float32
    )
    lat_own = lat_own.astype(jnp.bfloat16).reshape(-1, 2, half_width)
    lat_proj = lax.all_gather(lat_own, ("tok", "lat"), axis=0, tiled=True)
    lat_count = lat_proj.shape[0]
    lat_proj = lat_proj.reshape(lat_count, 2, head_count, head_size)
    per_head = (
        jnp.transpose(tok_proj[:, 0], (1, 0, 2)),
        jnp.transpose(tok_proj[:, 1], (1, 0, 2)),
        jnp.transpose(lat_proj[:, 0], (1, 0, 2)),
        jnp.transpose(lat_proj[:, 1], (1, 0, 2)),
    )
    tok_att, block_num, block_den, peaks = lax.map(head_terms, per_head)
    tok_att = jnp.transpose(tok_att, (1, 0, 2)).reshape(row_count, half_width)
    block_num = jnp.transpose(block_num, (1, 0, 2))
    block_den = jnp.transpose(block_den)
    peaks = jnp.transpose(peaks)
    got_num = lax.all_to_all(
        block_num.reshape(lat_count, half_width),
        ("tok", "lat"),
        split_axis=0,
        concat_axis=0,
        tiled=True,
    )
    got_den = lax.all_to_all(block_den, ("tok", "lat"), split_axis=0, concat_axis=0, tiled=True)
    got_peak = lax.all_to_all(peaks, ("tok", "lat"), split_axis=0, concat_axis=0, tiled=True)
    sources = lax.axis_size(("tok", "lat"))
    got_num = got_num.reshape(sources, -1, head_count, head_size)
    got_den = got_den.reshape(sources, -1, head_count)
    got_peak = got_peak.reshape(sources, -1, head_count)
    score_top = jnp.max(got_peak, axis=0)
    factor = jnp.exp(got_peak - score_top)
    num_own = jnp.sum(got_num * factor[:, :, :, None], axis=0)
    den_own = jnp.sum(got_den * factor, axis=0)
    lat_att = (num_own / den_own[:, :, None]).astype(jnp.bfloat16).reshape(-1, half_width)
    lat_part = jnp.dot(lat_att, o_lat[0], preferred_element_type=jnp.float32)
    lat_sum = lax.psum(lat_part, "rep")
    latents = (latents.astype(jnp.float32) + lat_sum).astype(jnp.bfloat16)
    tok_part = jnp.dot(tok_att, o_tok[0], preferred_element_type=jnp.float32)
    tok_sum = lax.psum(tok_part, "rep")
    tokens = (tokens.astype(jnp.float32) + tok_sum).astype(jnp.bfloat16)
    return (tokens, latents)

MESH_ID = pl.DeviceIdType.MESH
UP, DOWN, ACROSS, PARTNER = 0, 1, 2, 3
LANES = 128
VMEM_BYTES = 67_043_328


def arrival_order(depth, z):
    found = []
    for row in range(depth):
        far = abs(row - z)
        if far:
            found.append((far, 0, -row, row, 0))
        found.append((far + 1, 1, -row, row, 1))
    found.sort()
    return [(row, across) for *_, row, across in found]


def looked_up(table, z, n):
    total = 0
    for i, entries in enumerate(table):
        for j, entry in enumerate(entries):
            if entry:
                total = total + entry * ((z == i) & (n == j)).astype(jnp.int32)
    return total


def kernel(
    depth,
    wide,
    tok_hbm,
    lat_hbm,
    w_tok_hbm,
    w_lat_hbm,
    o_tok_hbm,
    o_lat_hbm,
    g_tok_hbm,
    g_lat_hbm,
    tok_out,
    lat_out,
    tok_all,
    lat_all,
    tok_own,
    lat_own,
    gain_ref,
    w_raw,
    w_ref,
    o_ref,
    query,
    peak,
    total,
    mixed,
    tok_att,
    lat_att,
    send_sem,
    recv_sem,
    load_sem,
    o_send,
    o_recv,
    att_send,
    att_recv,
):
    z = lax.axis_index("tok")
    x = lax.axis_index("lat")
    core = lax.axis_index("rep")
    across = 1 - x
    width = tok_all.shape[1]
    sizes = (lat_own.shape[0], tok_own.shape[0])
    half_width = w_raw.shape[3]
    head_size = D // HEADS
    pairs = half_width // LANES
    blocks = depth * wide
    me = z * wide + x
    bf16, f32 = jnp.bfloat16, jnp.float32
    devices = {
        UP: {"tok": z + 1},
        DOWN: {"tok": z - 1},
        ACROSS: {"lat": across},
        PARTNER: {"rep": 1 - core},
    }
    has_up = z + 1 < depth
    has_down = z > 0
    barrier = pltpu.get_barrier_semaphore()

    def greet(way):
        pl.semaphore_signal(barrier, inc=1, device_id=devices[way], device_id_type=MESH_ID)

    pl.when(has_down)(lambda: greet(DOWN))
    pl.when(has_up)(lambda: greet(UP))
    greet(ACROSS)
    greet(PARTNER)

    own = (lat_own, tok_own)
    gathered = (lat_all, tok_all)
    mine = pl.ds(pl.multiple_of(core * half_width, LANES), half_width)
    loads = [
        pltpu.make_async_copy(lat_hbm, lat_own, load_sem.at[0]),
        pltpu.make_async_copy(tok_hbm, tok_own, load_sem.at[1]),
        pltpu.make_async_copy(g_lat_hbm, gain_ref.at[0], load_sem.at[2]),
        pltpu.make_async_copy(g_tok_hbm, gain_ref.at[1], load_sem.at[3]),
        pltpu.make_async_copy(w_lat_hbm.at[0], w_raw.at[0], load_sem.at[4]),
        pltpu.make_async_copy(w_tok_hbm.at[0], w_raw.at[1], load_sem.at[5]),
        pltpu.make_async_copy(o_lat_hbm.at[0], o_ref.at[0, mine], load_sem.at[6]),
        pltpu.make_async_copy(o_tok_hbm.at[0], o_ref.at[1, mine], load_sem.at[7]),
    ]
    for load in loads:
        load.start()

    def block_rows(kind, block):
        return pl.ds(pl.multiple_of(block * sizes[kind], 16), sizes[kind])

    for kind in range(2):
        loads[kind].wait()
        loads[2 + kind].wait()
        gathered[kind][block_rows(kind, me), :] = rms_scale(own[kind][...], gain_ref[kind])

    pl.semaphore_wait(barrier, 2 + has_up.astype(jnp.int32) + has_down.astype(jnp.int32))

    def part(kind, block, half):
        rows = sizes[kind] // 2
        start = pl.multiple_of(block * sizes[kind] + half * rows, 16)
        return gathered[kind].at[pl.ds(start, rows)]

    def piece(kind, block, way):
        target = part(kind, block, core)
        return pltpu.make_async_remote_copy(
            src_ref=target,
            dst_ref=target,
            send_sem=send_sem.at[way, kind, block],
            recv_sem=recv_sem.at[core, kind, block],
            device_id=devices[way],
            device_id_type=MESH_ID,
        )

    def landed(kind, block, half):
        target = part(kind, block, half)
        pltpu.make_async_copy(target, target, recv_sem.at[half, kind, block]).wait()

    def own_ways(act):
        pl.when(has_down)(lambda: act(DOWN))
        pl.when(has_up)(lambda: act(UP))
        act(ACROSS)

    orders = [arrival_order(depth, row) for row in range(depth)]
    rows_table = [[row for row, _ in order] for order in orders]
    across_table = [[flag for _, flag in order] for order in orders]

    def arrival(n):
        row = looked_up(rows_table, z, n)
        crossed = looked_up(across_table, z, n)
        column = x + crossed * (across - x)
        return row, crossed, row * wide + column

    def relay_ways(row, crossed, act):
        straight = crossed == 0
        pl.when(straight & (row > z) & has_down)(lambda: act(DOWN))
        pl.when(straight & (row < z) & has_up)(lambda: act(UP))
        pl.when(straight)(lambda: act(ACROSS))
        act(PARTNER)

    def relay(n):
        row, crossed, block = arrival(n)
        for kind in range(2):
            landed(kind, block, core)
            relay_ways(row, crossed, lambda way: piece(kind, block, way).start())

    for kind in range(2):
        own_ways(lambda way: piece(kind, me, way).start())

    o_copies = [
        pltpu.make_async_remote_copy(
            src_ref=hbm.at[0],
            dst_ref=o_ref.at[i, mine],
            send_sem=o_send.at[i],
            recv_sem=o_recv.at[i],
            device_id=devices[PARTNER],
            device_id_type=MESH_ID,
        )
        for i, hbm in enumerate((o_lat_hbm, o_tok_hbm))
    ]
    for copy in o_copies:
        copy.start()

    def project(kind, block):
        both = jnp.dot(
            gathered[kind][block_rows(kind, block), :],
            w_ref[kind],
            preferred_element_type=f32,
        ).astype(bf16)
        return both[:, :half_width], both[:, half_width:]

    def attend(kind, key, value, first):
        for pair in range(pairs):
            lanes = slice(pair * LANES, (pair + 1) * LANES)
            scores = lax.dot_general(
                key[:, lanes],
                query[kind, pair],
                (((1,), (1,)), ((), ())),
                preferred_element_type=f32,
            )
            top = jnp.max(scores, axis=0, keepdims=True)
            if not first:
                old = peak[kind, pair]
                top = jnp.maximum(old, top)
            weights = jnp.exp(scores - top)
            added = jnp.sum(weights, axis=0, keepdims=True)
            product = lax.dot_general(
                value[:, lanes],
                weights.astype(bf16),
                (((0,), (0,)), ((), ())),
                preferred_element_type=f32,
            )
            span = product.shape[1] // 2
            upper = product[:head_size, :span]
            lower = product[head_size:, span:]
            base = pair * LANES
            if first:
                total[kind, pair] = added
                mixed[kind, base : base + head_size] = upper
                mixed[kind, base + head_size : base + LANES] = lower
            else:
                shrink = jnp.exp(old - top)
                total[kind, pair] = total[kind, pair] * shrink + added
                mixed[kind, base : base + head_size] = (
                    mixed[kind, base : base + head_size] * shrink[:, :span] + upper
                )
                mixed[kind, base + head_size : base + LANES] = (
                    mixed[kind, base + head_size : base + LANES] * shrink[:, span:] + lower
                )
            peak[kind, pair] = top

    for kind in range(2):
        loads[4 + kind].wait()
        w_ref[kind] = w_raw[kind].reshape(width, 2 * half_width)

    kept = []
    span = query.shape[2] // 2
    query[...] = jnp.zeros_like(query)
    for kind in range(2):
        key, value = project(kind, me)
        kept.append((key, value))
        scaled = key * jnp.asarray(head_size ** (-0.5), bf16)
        for pair in range(pairs):
            part_key = scaled[:, pair * LANES : (pair + 1) * LANES]
            leading = lax.broadcasted_iota(jnp.int32, part_key.shape, 1) < head_size
            zero = jnp.zeros_like(part_key)
            query[kind, pair, : sizes[kind]] = jnp.where(leading, part_key, zero)
            query[kind, pair, span : span + sizes[kind]] = jnp.where(leading, zero, part_key)
    for kind in range(2):
        attend(kind, *kept[1 - kind], True)

    def process(n):
        _, _, block = arrival(n)
        both = []
        for kind in range(2):
            landed(kind, block, 1 - core)
            both.append(project(kind, block))
        for kind in range(2):
            attend(kind, *both[1 - kind], False)

    def step(n, carry):
        pl.when(n < blocks - 1)(lambda: relay(n))
        pl.when(n > 0)(lambda: process(n - 1))
        return carry

    lax.fori_loop(0, blocks, step, 0)

    attended = (lat_att, tok_att)
    att_copies = []
    for kind in range(2):
        for pair in range(pairs):
            scale = 1.0 / total[kind, pair]
            base = pair * LANES
            attended[kind][core, base : base + head_size] = (
                mixed[kind, base : base + head_size] * scale[:, :span]
            ).astype(bf16)
            attended[kind][core, base + head_size : base + LANES] = (
                mixed[kind, base + head_size : base + LANES] * scale[:, span:]
            ).astype(bf16)
        copy = pltpu.make_async_remote_copy(
            src_ref=attended[kind].at[core],
            dst_ref=attended[kind].at[core],
            send_sem=att_send.at[kind],
            recv_sem=att_recv.at[kind],
            device_id=devices[PARTNER],
            device_id_type=MESH_ID,
        )
        copy.start()
        att_copies.append(copy)

    def mapped(kind, half):
        rows = pl.ds(pl.multiple_of(half * half_width, LANES), half_width)
        return lax.dot_general(
            attended[kind][half],
            o_ref[kind, rows, :],
            (((0,), (0,)), ((), ())),
            preferred_element_type=f32,
        )[: sizes[kind]]

    outs = (lat_out, tok_out)
    sums = []
    for kind in range(2):
        loads[6 + kind].wait()
        sums.append(own[kind][...].astype(f32) + mapped(kind, core))
    for kind in range(2):
        o_copies[kind].wait()
        att_copies[kind].wait()
        outs[kind][...] = (sums[kind] + mapped(kind, 1 - core)).astype(bf16)

    for kind in range(2):
        own_ways(lambda way: piece(kind, me, way).wait_send())

    def drain(n, carry):
        row, crossed, block = arrival(n)
        for kind in range(2):
            relay_ways(row, crossed, lambda way: piece(kind, block, way).wait_send())
        return carry

    lax.fori_loop(0, blocks - 1, drain, 0)


def gathered_body(tokens, latents, w_tok, w_lat, o_tok, o_lat, g_tok, g_lat):
    depth = lax.axis_size("tok")
    wide = lax.axis_size("lat")
    tok_rows, width = tokens.shape
    lat_rows = latents.shape[0]
    half_width = w_tok.shape[3]
    blocks = depth * wide
    pairs = half_width // LANES
    span = -(-max(tok_rows, lat_rows) // LANES) * LANES
    bf16, f32 = jnp.bfloat16, jnp.float32
    vmem = pl.BlockSpec(memory_space=pltpu.VMEM)
    hbm = pl.BlockSpec(memory_space=pltpu.MemorySpace.HBM)
    dma = pltpu.SemaphoreType.DMA
    return pl.pallas_call(
        functools.partial(kernel, depth, wide),
        out_shape=(
            jax.ShapeDtypeStruct(tokens.shape, bf16),
            jax.ShapeDtypeStruct(latents.shape, bf16),
        ),
        in_specs=[hbm] * 8,
        out_specs=(vmem, vmem),
        scratch_shapes=[
            pltpu.VMEM((blocks * tok_rows, width), bf16),
            pltpu.VMEM((blocks * lat_rows, width), bf16),
            pltpu.VMEM((tok_rows, width), bf16),
            pltpu.VMEM((lat_rows, width), bf16),
            pltpu.VMEM((2, 1, width), f32),
            pltpu.VMEM((2, width, 2, half_width), bf16),
            pltpu.VMEM((2, width, 2 * half_width), bf16),
            pltpu.VMEM((2, 2 * half_width, width), bf16),
            pltpu.VMEM((2, pairs, 2 * span, LANES), bf16),
            pltpu.VMEM((2, pairs, 1, 2 * span), f32),
            pltpu.VMEM((2, pairs, 1, 2 * span), f32),
            pltpu.VMEM((2, half_width, span), f32),
            pltpu.VMEM((2, half_width, span), bf16),
            pltpu.VMEM((2, half_width, span), bf16),
            dma((4, 2, blocks)),
            dma((2, 2, blocks)),
            dma((8,)),
            dma((2,)),
            dma((2,)),
            dma((2,)),
            dma((2,)),
        ],
        compiler_params=pltpu.CompilerParams(
            collective_id=0, has_side_effects=True, vmem_limit_bytes=VMEM_BYTES
        ),
    )(tokens, latents, w_tok, w_lat, o_tok, o_lat, g_tok, g_lat)


def solution(mesh):
    placed = (
        P(("groups", "tok", "lat"), None),
        P(("tok", "lat"), None),
        P(None, None, None, "rep"),
        P(None, None, None, "rep"),
        P(None, "rep", None),
        P(None, "rep", None),
        P(),
        P(),
    )
    sizes = dict(mesh.shape)
    resident = sizes["lat"] == 2 and sizes["rep"] == 2 and 2 <= sizes["tok"] <= 4
    return jax.shard_map(
        gathered_body if resident else body,
        mesh=mesh,
        in_specs=placed,
        out_specs=(P(("groups", "tok", "lat"), None), P(("groups", "tok", "lat"), None)),
        check_vma=False,
    )
```

time: 31.7 us -> 27.5 us (0.87)
  Pallas kernels: 27.1 us -> 24.3 us
  local copies, waits for them, and re-layouts: 3.53 us -> 2.25 us
    pallas_call x1, Pallas kernels: 27.1 us -> 24.3 us  [gathered_body(): pl.pallas_call(functools.partial(kernel, depth, wide), out_shape=(jax.Sha...]
    unnamed x18 -> x4, local copies, waits for them, and re-layouts: 3.53 us -> 2.25 us
where the time goes in v1:
time: 27.5 us; the launch traced here: 27.2 us
  Pallas kernels  24.3 us (88%)
  local copies, waits for them, and re-layouts  2.25 us (8%)
  between operations  0.65 us (2%)
    pallas_call x1, Pallas kernels, gathered_body(): pl.pallas_call(functools.partial(kernel, depth, wide), out_shape=(jax.Sha...  24.3 us
    unnamed x4, local copies, waits for them, and re-layouts  2.25 us

profile of v1, /device:TPU:1, one launch (start us, length us, event | category | flops | bytes accessed | tf_op | source)
XLA Modules:
  0.0 27.2 jit_solution(385205495820933392)
XLA Ops:
  0.6 24.3 %shard_map.95 = (bf16[128,512]{1,0:T(8,128)(2,1)}, bf16[96,512]{1,0:T(8,128)(2,1)}) custom-call(bf16[128,512]{1,0:T(8,128)(2,1)} %tok_hbm.1, bf16[96,512]{1,0:T(8,128)(2,1)} %lat_hbm.1, bf16[1,512,2,256]{3,2,1,0:T(2,128)(2,1)} %w_tok_hbm.1, bf16[1,512,2,256]{3,2,1,0:T(2,128)(2,1)} %w_lat_hbm.1, bf16[1,256,512]{2,1,0:T(8,128)(2,1)} %o_tok_hbm.1, ...), custom_call_target="tpu_custom_call" | custom-call | tf_op jit(solution)/shard_map/pallas_call | solution.py:434
  25.0 0.0 copy-start
  25.0 1.6 %copy.12 = bf16[128,512]{1,0:T(8,128)(2,1)} copy(bf16[128,512]{1,0:T(8,128)(2,1)} %get-tuple-element.4) | data formatting | bytes 262144
  26.6 0.0 copy-done
  26.6 0.6 %copy.13 = bf16[96,512]{1,0:T(8,128)(2,1)} copy(bf16[96,512]{1,0:T(8,128)(2,1)S(1)} %copy-done) | data formatting | bytes 196608
Async XLA Ops:
  25.0 1.6 %copy-start = (bf16[96,512]{1,0:T(8,128)(2,1)S(1)}, bf16[96,512]{1,0:T(8,128)(2,1)}, u32[]{:S(2)}) copy-start(bf16[96,512]{1,0:T(8,128)(2,1)} %get-tuple-element.5) | copy-start | bytes 294916
